TPU v7x, 512 devices: a whole 4x4x16 slice. The times are simulated.
512 devices in a mesh: sta: 32 (over z_lo, y), seg: 16 (over z_hi, x, core).
Axes of the slice: x: 4, y: 4, z: 16 (z_hi: 2, z_lo: 8; z = z_hi * 8 + z_lo), core: 2. Of those that a mesh axis runs over, the one named last changes fastest.
Arguments:
- spectra: bfloat16 [192, 64, 2, 1024], P('sta', 'seg'), may hold values from -6 to 6
- observed: float32 [544, 6, 6, 512], P('sta'), may hold values from -8 to 8
- pair_table: int32 [544, 2], P('sta'), may hold values from -1 to 31, as said below
Outputs:
- gradient: float32 [192, 2, 1024], P('sta', None, 'seg')
Inputs may be any that keep to these rules, and one draw needn't show every extreme that they name: `pair_table`: rows are slots; each unordered pair of station blocks p <= q of the 32 blocks stands in exactly one row as (p, q); every other row is (-1, -1).
All inputs are finite; a program needn't handle non-finite values.
Results may differ from a plain program's by a relative error of at most 0.0013.
Values may be sent and summed in bfloat16 or wider, within the bound.
A program may use at most 64 MiB of HBM per device.

v0:
```python
import math

import jax
import jax.numpy as jnp
from jax import lax
from jax.sharding import Mesh
from jax.sharding import PartitionSpec as P

F = 1024
LAGS = 512
SEG = ("seg_0", "seg_1", "seg_2")
STA = ("sta_0", "sta_1")


def cut_along(array, dim, length):
    before, after = (array.shape[:dim], array.shape[dim + 1 :])
    return jnp.moveaxis(array.reshape(*before, length, -1, *after), dim, 0)


def laid_out(pieces, dim):
    shape = list(pieces.shape[1:])
    shape[dim] *= pieces.shape[0]
    return jnp.moveaxis(pieces, 0, dim).reshape(shape)


def turned_blocks(pieces, axes, turns):
    shape = [lax.axis_size(a) for a in axes]
    pieces = pieces.reshape(*shape, *pieces.shape[1:])
    for k in turns:
        pieces = lax.all_to_all(pieces, axes[k], split_axis=k, concat_axis=k, tiled=True)
    return pieces.reshape(-1, *pieces.shape[len(axes) :])


def core_and_chips(array, groups, turns, split_dim, concat_dim):
    length = lax.axis_size(groups[0]) * lax.axis_size(groups[1])
    pieces = cut_along(array, split_dim, length)
    return laid_out(turned_blocks(pieces, groups, turns), concat_dim)


def all_blocks(array, axes, turns):
    pieces = array
    for k in turns:
        pieces = lax.all_gather(pieces, axes[k])
    done = turns[::-1]
    back = [done.index(k) for k in range(len(axes))]
    pieces = pieces.transpose(*back, *range(len(axes), pieces.ndim))
    return pieces.reshape(-1, *array.shape)


def gather_axes(array, axes, turns, dim):
    return laid_out(all_blocks(array, axes, turns), dim)


def sent_and_summed(array, axis, dim):
    pieces = cut_along(array, dim, lax.axis_size(axis))
    arrived = lax.all_to_all(pieces, axis, split_axis=0, concat_axis=0, tiled=True)
    return arrived.sum(axis=0)


def lag_kernel(count):
    frequency = jnp.arange(count, dtype=jnp.int32)[:, None]
    offset = jnp.arange(LAGS, dtype=jnp.int32)[None, :] - LAGS // 2
    phase = jnp.mod(frequency * offset, 2 * F)
    angle = math.pi / F * phase.astype(jnp.float32)
    return jnp.stack([jnp.cos(angle), -jnp.sin(angle)], axis=0).astype(jnp.bfloat16)


def group_cross(left, right, groups):
    station_count = left.shape[0]
    left = left.reshape(station_count, groups, -1, 2, left.shape[-1]).astype(jnp.float32)
    right = right.reshape(station_count, groups, -1, 2, right.shape[-1]).astype(jnp.float32)
    left_real = left[:, :, :, 0][:, None]
    left_imag = left[:, :, :, 1][:, None]
    right_real = right[:, :, :, 0][None]
    right_imag = right[:, :, :, 1][None]
    cross_real = jnp.sum(left_real * right_real + left_imag * right_imag, axis=3)
    cross_imag = jnp.sum(left_imag * right_real - left_real * right_imag, axis=3)
    return jnp.stack([cross_real, cross_imag], axis=3).astype(jnp.bfloat16)


def slot_cross(gathered, starts_all, station_count, groups):

    def one_slot(starts):
        left = lax.dynamic_slice_in_dim(gathered, starts[0], station_count, 0)
        right = lax.dynamic_slice_in_dim(gathered, starts[1], station_count, 0)
        return group_cross(left, right, groups)

    return lax.map(one_slot, starts_all)


def pair_mask(first, second, station_count):
    row_index = jnp.arange(station_count)[:, None]
    col_index = jnp.arange(station_count)[None, :]
    keep = (first >= 0)[..., None, None] & (
        (first != second)[..., None, None] | (row_index < col_index)
    )
    return keep.astype(jnp.float32)


def on_device(spectra, observed, pair_table):
    station_dev = spectra.shape[0]
    slot_count = pair_table.shape[0]
    seg_devices = lax.axis_size(SEG)
    scale = 1.0 / math.sqrt(F * spectra.shape[1] * seg_devices)
    first = pair_table[:, 0]
    second = pair_table[:, 1]
    starts_all = jnp.maximum(pair_table, 0) * station_dev
    keep = pair_mask(first, second, station_dev).reshape(-1, 1)
    observe_flat = observed.reshape(-1, LAGS)
    local = core_and_chips(spectra, (("seg_0", "seg_1"), "seg_2"), (1, 0), 3, 1)
    gathered = gather_axes(local, STA, (0, 1), 0)
    width = local.shape[3]
    crossed = slot_cross(gathered, starts_all, station_dev, seg_devices)
    stacked = jnp.sum(lax.optimization_barrier(crossed).astype(jnp.float32), axis=3)
    total_rows = slot_count * station_dev * station_dev
    share_rows = -(-total_rows // seg_devices)
    padding = share_rows * seg_devices - total_rows
    flat = jnp.pad(stacked.reshape(total_rows, 2, width), ((0, padding), (0, 0), (0, 0)))
    owned = lax.all_to_all(flat, SEG, split_axis=0, concat_axis=2, tiled=True)
    row_start = lax.axis_index(SEG) * share_rows
    keep_rows = lax.dynamic_slice_in_dim(
        jnp.pad(keep, ((0, padding), (0, 0))), row_start, share_rows, 0
    )
    observe_rows = lax.dynamic_slice_in_dim(
        jnp.pad(observe_flat, ((0, padding), (0, 0))), row_start, share_rows, 0
    )
    kernel = lag_kernel(F)
    exact = lax.optimization_barrier(kernel).astype(jnp.float32).reshape(2 * F, LAGS)
    lags = scale * jnp.dot(owned.reshape(share_rows, 2 * F), exact, precision=lax.Precision.HIGHEST)
    residual = (keep_rows * jnp.tanh(lags - observe_rows)).astype(jnp.bfloat16)
    gamma = scale * lax.dot_general(
        residual,
        kernel.reshape(2 * F, LAGS),
        (((1,), (1,)), ((), ())),
        preferred_element_type=jnp.float32,
    )
    gamma = gamma.reshape(share_rows, 2, F)
    common = gamma[:, 0] * owned[:, 0] + gamma[:, 1] * owned[:, 1]
    twist = gamma[:, 1] * owned[:, 0] - gamma[:, 0] * owned[:, 1]
    returned = lax.all_to_all(
        jnp.stack([common, twist], axis=1), SEG, split_axis=2, concat_axis=0, tiled=True
    )
    returned = returned[:total_rows].reshape(slot_count, station_dev, station_dev, 2, width)
    common_all = returned[:, :, :, 0]
    twist_all = returned[:, :, :, 1]
    left_term = jnp.stack([common_all.sum(2), twist_all.sum(2)], axis=-2)
    right_term = jnp.stack([common_all.sum(1), -twist_all.sum(1)], axis=-2)
    blocks = lax.axis_size(STA)
    block_index = jnp.arange(blocks)[None, :]
    choose_left = (first[:, None] == block_index).astype(jnp.float32)
    choose_right = (second[:, None] == block_index).astype(jnp.float32)
    contract = (((0,), (0,)), ((), ()))
    buffer = lax.dot_general(
        choose_left, left_term.reshape(slot_count, -1), contract, precision=lax.Precision.HIGHEST
    )
    buffer = buffer + lax.dot_general(
        choose_right, right_term.reshape(slot_count, -1), contract, precision=lax.Precision.HIGHEST
    )
    buffer = buffer.reshape(blocks * station_dev, 2, width)
    result = sent_and_summed(buffer, STA, 0)
    return result


def solution(mesh):
    torus = Mesh(mesh.devices.reshape(8, 4, 2, 4, 2), ("sta_0", "sta_1", "seg_0", "seg_1", "seg_2"))
    in_specs = (P(STA, SEG, None, None), P(STA, None, None, None), P(STA, None))
    out_specs = P(STA, None, SEG)
    return jax.shard_map(
        on_device, mesh=torus, in_specs=in_specs, out_specs=out_specs, check_vma=False
    )
```

profile of v0, /device:TPU:1, one launch (start us, length us, event | category | flops | bytes accessed | tf_op | source)
XLA Modules:
  0.0 425.5 jit_solution(2719285432693006553)
XLA Ops:
  6.5 1.1 reshape.266
  7.9 10.3 %all_to_all.51 = bf16[2,2,12288]{2,1,0:T(2,128)(2,1)S(1)} all-to-all(bf16[2,2,12288]{2,1,0:T(2,128)(2,1)S(1)} %reshape.280), channel_id=1, replica_groups=mesh['sta_0'=8,'sta_1'=4,'seg_0'=2,'seg_1'=4,'seg_2'=2] {'seg_2'}, dimensions={0} | all-to-all | bytes 196608 | tf_op jit(solution)/shard_map/all_to_all | solution.py:30
  18.7 25.7 %all_to_all.52 = bf16[8,2,3072]{2,1,0:T(2,128)(2,1)S(1)} all-to-all(bf16[8,2,3072]{2,1,0:T(2,128)(2,1)S(1)} %reshape.282), channel_id=1, replica_groups=mesh['sta_0'=8,'sta_1'=4,'seg_0'=2,'seg_1'=4,'seg_2'=2] {'seg_0','seg_1'}, dimensions={0} | all-to-all | bytes 196608 | tf_op jit(solution)/shard_map/all_to_all | solution.py:30
  44.9 49.0 %all_gather.9 = bf16[8,6,64,2,64]{4,2,3,1,0:T(8,128)(2,1)} all-gather(bf16[1,6,64,2,64]{4,2,3,1,0:T(8,128)(2,1)S(1)} %bitcast.120), channel_id=1, replica_groups=mesh['sta_0'=8,'sta_1'=4,'seg_0'=2,'seg_1'=4,'seg_2'=2] {'sta_0'}, dimensions={0}, use_global_device_ids=true | all-gather | bytes 884736 | tf_op jit(solution)/shard_map/all_gather | solution.py:43
  93.9 72.9 %all-gather.3.cloned.1.call-done = bf16[32,6,64,2,64]{4,2,3,1,0:T(8,128)(2,1)} async-done(((bf16[8,6,64,2,64]{4,2,3,1,0:T(8,128)(2,1)}), bf16[32,6,64,2,64]{4,2,3,1,0:T(8,128)(2,1)}) %all-gather.3.cloned.1.call-update) | async-done | bytes 3145744 | tf_op jit(solution)/shard_map/all_gather | solution.py:43
  166.8 4.3 %copy.52 = bf16[8,4,6,64,2,64]{5,3,4,2,1,0:T(8,128)(2,1)S(1)} copy(bf16[8,4,6,64,2,64]{5,3,4,2,0,1:T(8,128)(2,1)} %bitcast.110) | data formatting | bytes 6291456 | tf_op jit(solution)/shard_map/transpose | solution.py:46
  171.1 6.3 %copy.53 = bf16[192,64,2,64]{3,2,1,0:T(2,128)(2,1)} copy(bf16[192,64,2,64]{3,1,2,0:T(8,128)(2,1)S(1)} %bitcast.101) | data formatting | bytes 6291456 | tf_op jit(solution)/shard_map/while | solution.py:88
  177.4 127.1 %while.10 = (s32[]{:T(128)}, bf16[17,6,6,16,2,64]{5,3,2,1,4,0:T(8,128)(2,1)}, s32[17,2]{0,1:T(2,128)S(1)}, bf16[192,64,2,64]{3,2,1,0:T(2,128)(2,1)}, s32[]{:T(128)}, /*index=5*/s32[]{:T(128)}, s32[]{:T(128)}) while((s32[]{:T(128)}, bf16[17,6,6,16,2,64]{5,3,2,1,4,0:T(8,128)(2,1)}, s32[17,2]{0,1:T(2,128)S(1)}, ...), condition=%wide.region_3.4_spmd, body=%wide.region_0.3_spmd.sunk | while | flops 1400840 | bytes 2949821 | solution.py:88
  181.6 1.4 constant_dynamic-slice_fusion.6
  184.1 0.8 maximum_dynamic-update-slice_fusion.2
  189.1 1.4 constant_dynamic-slice_fusion.6
  191.6 0.8 maximum_dynamic-update-slice_fusion.2
  196.6 1.4 constant_dynamic-slice_fusion.6
  199.1 0.8 maximum_dynamic-update-slice_fusion.2
  204.0 1.4 constant_dynamic-slice_fusion.6
  206.5 0.8 maximum_dynamic-update-slice_fusion.2
  211.5 1.4 constant_dynamic-slice_fusion.6
  214.0 0.8 maximum_dynamic-update-slice_fusion.2
  219.0 1.4 constant_dynamic-slice_fusion.6
  221.5 0.8 maximum_dynamic-update-slice_fusion.2
  226.4 1.4 constant_dynamic-slice_fusion.6
  229.0 0.8 maximum_dynamic-update-slice_fusion.2
  233.9 1.4 constant_dynamic-slice_fusion.6
  236.4 0.8 maximum_dynamic-update-slice_fusion.2
  241.4 1.4 constant_dynamic-slice_fusion.6
  243.9 0.8 maximum_dynamic-update-slice_fusion.2
  248.9 1.4 constant_dynamic-slice_fusion.6
  251.4 0.8 maximum_dynamic-update-slice_fusion.2
  256.4 1.4 constant_dynamic-slice_fusion.6
  258.9 0.8 maximum_dynamic-update-slice_fusion.2
  263.9 1.4 constant_dynamic-slice_fusion.6
  266.4 0.8 maximum_dynamic-update-slice_fusion.2
  271.3 1.4 constant_dynamic-slice_fusion.6
  273.9 0.8 maximum_dynamic-update-slice_fusion.2
  278.8 1.4 constant_dynamic-slice_fusion.6
  281.3 0.8 maximum_dynamic-update-slice_fusion.2
  286.3 1.4 constant_dynamic-slice_fusion.6
  288.8 0.8 maximum_dynamic-update-slice_fusion.2
  293.8 1.4 constant_dynamic-slice_fusion.6
  296.3 0.8 maximum_dynamic-update-slice_fusion.2
  301.3 1.4 constant_dynamic-slice_fusion.6
  303.8 0.8 maximum_dynamic-update-slice_fusion.2
  304.6 4.8 %convert_reduce_fusion = f32[17,6,6,2,64]{4,2,1,3,0:T(8,128)S(1)} fusion(bf16[17,6,6,16,2,64]{5,3,2,1,4,0:T(8,128)(2,1)} %get-tuple-element.27), kind=kLoop, calls=%fused_computation.8 | loop fusion | flops 2428416 | bytes 2820096 | tf_op jit(solution)/shard_map/reduce_sum | solution.py:114
  309.9 1.4 reshape.284
  311.3 15.5 %all-to-all-start.2 = ((f32[16,1,4992]{2,1,0:T(1,128)}), f32[16,1,4992]{2,1,0:T(1,128)S(1)}, u32[]{:S(2)}, u32[]{:S(2)}) async-start(f32[16,1,4992]{2,1,0:T(1,128)} %reshape.284), calls=%async_computation.2 | async-start | bytes 638976 | tf_op jit(solution)/shard_map/all_to_all | solution.py:119
  327.0 8.6 %fusion.10 = (bf16[1,1024,512]{2,1,0:T(8,128)(2,1)S(1)}, bf16[1,1024,512]{2,1,0:T(8,128)(2,1)S(1)}) fusion(s32[512]{0:T(512)S(1)} %iota_add_fusion), kind=kLoop, calls=%fused_computation.28 | loop fusion | flops 8912896 | bytes 2099200 | tf_op jit(solution)/shard_map/cos | solution.py:65
  335.9 2.5 reshape.272
  338.5 5.3 %all-to-all-done.2 = f32[16,1,4992]{2,1,0:T(1,128)S(1)} async-done(((f32[16,1,4992]{2,1,0:T(1,128)}), f32[16,1,4992]{2,1,0:T(1,128)S(1)}, u32[]{:S(2)}, u32[]{:S(2)}) %all-to-all-start.2) | async-done | bytes 319520 | tf_op jit(solution)/shard_map/all_to_all | solution.py:119
  344.3 1.4 reduce.4
  346.1 0.9 copy.80
  347.1 1.3 reshape.270
  348.4 2.0 fusion.9
  350.4 0.7 convolution_multiply_fusion
  352.0 0.6 copy.60
  352.6 2.5 reshape.286
  355.1 9.1 %all-to-all-start.3 = ((f32[16,1,4992]{2,1,0:T(1,128)}), f32[16,1,4992]{2,1,0:T(1,128)S(1)}, u32[]{:S(2)}, u32[]{:S(2)}) async-start(f32[16,1,4992]{2,1,0:T(1,128)} %reshape.286), calls=%async_computation.3 | async-start | bytes 638976 | tf_op jit(solution)/shard_map/all_to_all | solution.py:140
  364.3 16.9 %all-to-all-done.3 = f32[16,1,4992]{2,1,0:T(1,128)S(1)} async-done(((f32[16,1,4992]{2,1,0:T(1,128)}), f32[16,1,4992]{2,1,0:T(1,128)S(1)}, u32[]{:S(2)}, u32[]{:S(2)}) %all-to-all-start.3) | async-done | bytes 319520 | tf_op jit(solution)/shard_map/all_to_all | solution.py:140
  381.2 1.4 reduce.5
  382.6 1.7 reshape.287
  384.2 0.6 copy.68
  385.3 1.3 slice_reduce_fusion.2
  388.3 28.6 %all_to_all.53 = f32[32,1,768]{2,1,0:T(1,128)S(1)} all-to-all(f32[32,1,768]{2,1,0:T(1,128)S(1)} %reshape.288), channel_id=1, replica_groups=mesh['sta_0'=8,'sta_1'=4,'seg_0'=2,'seg_1'=4,'seg_2'=2] {'sta_0','sta_1'}, dimensions={0} | all-to-all | bytes 196608 | tf_op jit(solution)/shard_map/all_to_all | solution.py:56
  416.9 0.9 reduce.6
  417.9 0.7 reduce_sum.77
  (202 shorter events, 35.3 us)
Async XLA Ops:
  6.5 160.3 %all-gather.3.cloned.1.call-start = ((), (), s32[]{:S(2)}) async-start(), calls=%async_computation.5 | async-start | bytes 7864320 | tf_op jit(solution)/shard_map/all_gather | solution.py:43
  44.6 49.3 %copy-start = (s32[17,2]{0,1:T(2,128)S(1)}, s32[17,2]{0,1:T(2,128)}, u32[]{:S(2)}) copy-start(s32[17,2]{0,1:T(2,128)} %param.7) | copy-start | bytes 412
  311.3 32.4 %all-to-all-start.2 = ((f32[16,1,4992]{2,1,0:T(1,128)}), f32[16,1,4992]{2,1,0:T(1,128)S(1)}, u32[]{:S(2)}, u32[]{:S(2)}) async-start(f32[16,1,4992]{2,1,0:T(1,128)} %reshape.284), calls=%async_computation.2 | async-start | bytes 638976 | tf_op jit(solution)/shard_map/all_to_all | solution.py:119
  355.1 26.0 %all-to-all-start.3 = ((f32[16,1,4992]{2,1,0:T(1,128)}), f32[16,1,4992]{2,1,0:T(1,128)S(1)}, u32[]{:S(2)}, u32[]{:S(2)}) async-start(f32[16,1,4992]{2,1,0:T(1,128)} %reshape.286), calls=%async_computation.3 | async-start | bytes 638976 | tf_op jit(solution)/shard_map/all_to_all | solution.py:140
Sparse Core Ops, SparseCore 0:
  94.0 72.7 all-gather.2
where the time goes:
time: 427 us; the launch traced here: 425 us
  blocking collectives  114 us (27%)
  waiting for transfers between devices  95.1 us (22%)
  local copies, waits for them, and re-layouts  72.9 us (17%)
  loops' own time  61.8 us (14%)
  other arithmetic  40.3 us (9%)
  starting transfers between devices  24.6 us (6%)
  between operations  13.8 us (3%)
    all_gather x1, waiting for transfers between devices, all_blocks(): pieces = lax.all_gather(pieces, axes[k])  72.9 us
    another operation x1, loops' own time, slot_cross(): return lax.map(one_slot, starts_all)  61.8 us
    all_gather x1, blocking collectives, all_blocks(): pieces = lax.all_gather(pieces, axes[k])  49 us
    all_to_all x2, blocking collectives, turned_blocks(): lax.all_to_all(pieces, axes[k], split_axis=k, concat_axis=k, tiled=True)  36 us
    all_to_all x1, blocking collectives, sent_and_summed(): lax.all_to_all(pieces, axis, split_axis=0, concat_axis=0, tiled=True)  28.6 us
    dynamic_slice x17, local copies, waits for them, and re-layouts, one_slot(): left = lax.dynamic_slice_in_dim(gathered, starts[0], station_count, 0)  22.9 us
    all_to_all x1, waiting for transfers between devices, on_device(): lax.all_to_all(jnp.stack([common, twist], axis=1), SEG, split_axis=2, con...  16.9 us
    all_to_all x1, starting transfers between devices, on_device(): owned = lax.all_to_all(flat, SEG, split_axis=0, concat_axis=2, tiled=True)  15.5 us
  transfers between devices with their start and end apart: 3, of which 3 were waited for; matrix products, arithmetic and copies ran while one was open for 3% of the time, Pallas kernels for 0%

commit v1 on v0

v1 whole, which is shorter than its diff:
```python
import math

import jax
import jax.numpy as jnp
from jax import lax
from jax.experimental import pallas as pl
from jax.experimental.pallas import tpu as pltpu
from jax.sharding import Mesh
from jax.sharding import PartitionSpec as P

F = 1024
LAGS = 512
STA_DEV = 6
SEGS = 64
SEG = ("seg_0", "seg_1", "seg_2")
STA = ("sta_0", "sta_1")
SCALE = 1.0 / math.sqrt(F * SEGS)
NEAR = 8
FAR = 64
F32 = jnp.float32
BF16 = jnp.bfloat16
NT = (((1,), (1,)), ((), ()))


def lag_kernel():
    frequency = jnp.arange(F, dtype=jnp.int32)[:, None]
    offset = jnp.arange(LAGS, dtype=jnp.int32)[None, :] - LAGS // 2
    phase = jnp.mod(frequency * offset, 2 * F)
    angle = math.pi / F * phase.astype(F32)
    kernel = jnp.stack([jnp.cos(angle), -jnp.sin(angle)], axis=0).astype(BF16)
    kernel = kernel.reshape(2, 2, 4, 2, 64, LAGS).transpose(3, 0, 2, 1, 4, 5)
    return kernel.reshape(4, 512, LAGS)


def far_id(index):
    return {"seg_0": index // 32, "sta_0": (index // 4) % 8, "sta_1": index % 4}


def near_id(index):
    return {"seg_1": index // 2, "seg_2": index % 2}


def exchange(count, me, device_of, source, target, send_sems, recv_sems):
    def copy_to(peer):
        return pltpu.make_async_remote_copy(
            src_ref=source(peer),
            dst_ref=target(me),
            send_sem=send_sems.at[peer],
            recv_sem=recv_sems.at[me],
            device_id=device_of(peer),
            device_id_type=pl.DeviceIdType.MESH,
        )

    def arrival_of(peer):
        return pltpu.make_async_remote_copy(
            src_ref=source(peer),
            dst_ref=target(peer),
            send_sem=send_sems.at[peer],
            recv_sem=recv_sems.at[peer],
            device_id=device_of(peer),
            device_id_type=pl.DeviceIdType.MESH,
        )

    def each(action):
        def step(i, carry):
            action(lax.rem(me + i, count))
            return carry

        lax.fori_loop(1, count, step, 0)

    each(lambda peer: copy_to(peer).start())
    return (
        lambda: each(lambda peer: arrival_of(peer).wait_recv()),
        lambda: each(lambda peer: copy_to(peer).wait_send()),
    )


def lane_iota(shape):
    return lax.broadcasted_iota(jnp.int32, shape, len(shape) - 1)


def body(
    x_ref, table_ref, pairs_ref, observed_ref, kernel_ref, out_ref,
    recv_a, send_b, recv_c, stage_b, stage_g, gram_m, onehot,
    stage_f, send_f, recv_f, send_g, recv_g, s_ref, send_i, recv_i, send_k, recv_k,
    obs_v, kern_v, local_sems, near_sems, far_sems,
):
    zh = lax.axis_index("seg_0")
    far = zh * 32 + lax.axis_index("sta_0") * 4 + lax.axis_index("sta_1")
    near = lax.axis_index("seg_1") * 2 + lax.axis_index("seg_2")
    seg = zh * 8 + near

    loads = [
        pltpu.make_async_copy(observed_ref.at[seg], obs_v.at[pl.ds(0, 6)], local_sems.at[0]),
        pltpu.make_async_copy(
            observed_ref.at[16, jnp.minimum(near, 5)], obs_v.at[6], local_sems.at[1]
        ),
        pltpu.make_async_copy(kernel_ref, kern_v, local_sems.at[2]),
    ]
    for load in loads:
        load.start()

    barrier = pltpu.get_barrier_semaphore()

    def greet(count, me, device_of):
        def step(i, carry):
            pl.semaphore_signal(
                barrier, inc=1, device_id=device_of(lax.rem(me + i, count)),
                device_id_type=pl.DeviceIdType.MESH,
            )
            return carry

        lax.fori_loop(1, count, step, 0)

    greet(FAR, far, far_id)
    greet(NEAR, near, near_id)
    pl.semaphore_wait(barrier, FAR + NEAR - 2)

    wait_a, sent_a = exchange(
        NEAR, near, near_id,
        lambda peer: x_ref.at[:, pl.ds(pl.multiple_of(peer * 128, 128), 128)],
        lambda peer: recv_a.at[peer],
        near_sems.at[0], near_sems.at[1],
    )
    recv_a[near] = x_ref[:, pl.ds(pl.multiple_of(near * 128, 128), 128)]
    stage_b[pl.ds(6, FAR, stride=8), :] = jnp.broadcast_to(table_ref[0:1, :], (FAR, 128))
    stage_b[pl.ds(7, FAR, stride=8), :] = jnp.broadcast_to(table_ref[1:2, :], (FAR, 128))
    wait_a()

    for pair in range(3):
        rows = []
        for a in (2 * pair, 2 * pair + 1):
            for m in range(NEAR):
                rows.append(recv_a[m].astype(F32)[8 * a : 8 * a + 8])
        turned = jnp.concatenate(rows, axis=0).T
        for fi in range(2):
            stage_b[pl.ds(3 * fi + pair, FAR, stride=8), :] = turned[64 * fi : 64 * fi + 64]
    send_b[...] = stage_b[...].reshape(FAR, 8, 128).astype(BF16)
    wait_c, sent_c = exchange(
        FAR, far, far_id,
        lambda peer: send_b.at[peer], lambda peer: recv_c.at[peer],
        far_sems.at[0], far_sems.at[1],
    )
    recv_c[far] = send_b[far]
    wait_c()
    stage_b[...] = recv_c[...].astype(F32).reshape(FAR * 8, 128)

    lane32 = lane_iota((32, 128))
    for fi in range(2):
        stations = []
        for pair in range(3):
            both = stage_b[pl.ds(3 * fi + pair, FAR, stride=8), :]
            low, high = both[0:32], both[32:64]
            stations.append(jnp.where(lane32 < 64, low, pltpu.roll(high, 64, 1)))
            stations.append(jnp.where(lane32 < 64, pltpu.roll(low, 64, 1), high))
        stations += [jnp.zeros((32, 128), F32)] * 2
        plain = jnp.concatenate(stations, axis=0)
        even = lax.rem(lane_iota((256, 128)), 2) == 0
        turned = jnp.where(even, pltpu.roll(plain, 127, 1), -pltpu.roll(plain, 1, 1))
        right = plain.astype(BF16)
        for c, left in enumerate((right, turned.astype(BF16))):
            gram = lax.dot_general(right, left, NT, preferred_element_type=F32)
            at = 256 * (2 * fi + c)
            stage_g[0, at : at + 256, :] = gram[:, 0:128]
            stage_g[1, at : at + 256, :] = gram[:, 128:256]

    for a in range(STA_DEV):
        for tile in range(8):
            kept = None
            for i in range(4):
                piece = stage_g[a // 4, pl.ds(4 * tile + i, 32, stride=32), :]
                shift = 32 * ((i - a) % 4)
                piece = pltpu.roll(piece, shift, 1) if shift else piece
                kept = piece if kept is None else jnp.where(lane32 >= 32 * i, piece, kept)
            gram_m[32 * a : 32 * a + 32, 128 * tile : 128 * tile + 128] = kept.astype(BF16)
    gram_m[192:256, :] = jnp.zeros((64, 1024), BF16)

    first = stage_b[pl.ds(6, FAR, stride=8), :]
    second = stage_b[pl.ds(7, FAR, stride=8), :]
    key = (second * 32.0 + first).astype(jnp.int32)
    row64 = lax.broadcasted_iota(jnp.int32, (FAR, 128), 0)
    main_key = jnp.where(row64 < 32, key, pltpu.roll(key, 120, 1))
    rest_key = jnp.where(row64 < 32, key, -1)
    lane1024 = lane_iota((FAR, 1024))
    for m in range(NEAR + 1):
        column = rest_key[:, 16:17] if m == NEAR else main_key[:, m : m + 1]
        hit = jnp.where(lane1024 == column, 1.0, 0.0)
        onehot[64 * m : 64 * m + 64, :] = hit.astype(BF16)
    slots = lax.dot_general(onehot[...], gram_m[...], NT, preferred_element_type=F32)
    lane64 = lane_iota((FAR, 128))
    for m in range(NEAR):
        stage_f[pl.ds(m, FAR, stride=16), :] = slots[64 * m : 64 * m + 64, 0:128]
        upper = slots[64 * m : 64 * m + 64, 128:256]
        if m < STA_DEV:
            rest = slots[512:576, 128 * (m // 4) : 128 * (m // 4) + 128]
            shift = (64 - 32 * (m % 4)) % 128
            rest = pltpu.roll(rest, shift, 1) if shift else rest
            upper = jnp.where(lane64 < 64, upper, jnp.where(lane64 < 96, rest, 0.0))
        stage_f[pl.ds(8 + m, FAR, stride=16), :] = upper
    send_f[...] = stage_f[...].astype(BF16)

    def chunk16(ref):
        return lambda peer: ref.at[pl.ds(pl.multiple_of(peer * 16, 16), 16), :]

    wait_f, sent_f = exchange(
        FAR, far, far_id, chunk16(send_f), chunk16(recv_f), far_sems.at[2], far_sems.at[3]
    )
    own = pl.ds(pl.multiple_of(far * 16, 16), 16)
    recv_f[own, :] = send_f[own, :]
    wait_f()
    stage_f[...] = recv_f[...].astype(F32)
    for m in range(NEAR):
        for t in range(2):
            part = stage_f[pl.ds(8 * t + m, FAR, stride=16), :]
            send_g[m, :, 128 * t : 128 * t + 128] = part.astype(BF16)
    wait_g, sent_g = exchange(
        NEAR, near, near_id,
        lambda peer: send_g.at[peer], lambda peer: recv_g.at[peer],
        near_sems.at[2], near_sems.at[3],
    )
    recv_g[near] = send_g[near]
    wait_g()

    for xt in range(4):
        low = recv_g[xt].astype(F32)
        high = recv_g[4 + xt].astype(F32)
        for t in range(2):
            square = jnp.concatenate(
                [low[:, 128 * t : 128 * t + 128], high[:, 128 * t : 128 * t + 128]], axis=0
            ).T
            for part in range(4 if t == 0 else 3):
                a = 4 * t + part
                for fc in range(4):
                    at = 32 * part + 8 * fc
                    s_ref[fc, 8 * a : 8 * a + 8, 128 * xt : 128 * xt + 128] = square[at : at + 8]
    for load in loads:
        load.wait()
    lags = jnp.zeros((56, LAGS), F32)
    for fc in range(4):
        lags = lags + jnp.dot(s_ref[fc].astype(BF16), kern_v[fc], preferred_element_type=F32)
    b_index = lax.broadcasted_iota(jnp.int32, (STA_DEV, LAGS), 0)
    rows = []
    for a in range(7):
        slot = seg if a < 6 else 16
        p, q = pairs_ref[slot, 0], pairs_ref[slot, 1]
        floor = jnp.where(p < 0, 99, jnp.where(p != q, -1, a if a < 6 else near))
        if a == 6:
            floor = jnp.where((zh == 0) & (near < 6), floor, 99)
        value = jnp.tanh(SCALE * lags[8 * a : 8 * a + 6] - obs_v[a])
        value = jnp.where(b_index > floor, value, 0.0)
        rows += [value, jnp.zeros((2, LAGS), F32)]
    residual = jnp.concatenate(rows, axis=0).astype(BF16)

    for fi in range(2):
        gamma = [
            SCALE * lax.dot_general(residual, kern_v[2 * fi + c], NT, preferred_element_type=F32)
            for c in range(2)
        ]
        s0, s1 = s_ref[2 * fi], s_ref[2 * fi + 1]
        common = gamma[0] * s0 + gamma[1] * s1
        twist = gamma[1] * s0 - gamma[0] * s1
        for ct, term in enumerate((common, twist)):
            left = [jnp.sum(term[8 * a : 8 * a + 8], axis=0, keepdims=True) for a in range(7)]
            left = jnp.concatenate(left + [jnp.zeros((1, 512), F32)], axis=0)
            right = term[0:8]
            for a in range(1, 6):
                right = right + term[8 * a : 8 * a + 8]
            for i, block in enumerate((left, right, term[48:56])):
                at = 24 * ct + 8 * i
                for xt in range(4):
                    send_i[2 * xt + fi, at : at + 8, :] = block[:, 128 * xt : 128 * xt + 128]
    wait_i, sent_i = exchange(
        NEAR, near, near_id,
        lambda peer: send_i.at[peer], lambda peer: recv_i.at[peer],
        near_sems.at[4], near_sems.at[5],
    )
    recv_i[near] = send_i[near]

    lane = lane_iota((1, 192))
    target = jnp.full((1, 192), -1, jnp.int32)
    sign = jnp.full((1, 192), 1.0, F32)
    rest_p = jnp.where(zh == 0, pairs_ref[16, 0], -1) * 8
    rest_q = jnp.where(zh == 0, pairs_ref[16, 1], -1) * 8
    for m in range(NEAR):
        t = lane - 24 * m
        p = pairs_ref[zh * 8 + m, 0] * 8
        q = pairs_ref[zh * 8 + m, 1] * 8
        value = jnp.where(t < 6, p + t, -1)
        value = jnp.where((t >= 8) & (t < 14), q + t - 8, value)
        if m < 6:
            value = jnp.where(t == 6, rest_p + m, value)
            value = jnp.where((t >= 16) & (t < 22), rest_q + t - 16, value)
        inside = (t >= 0) & (t < 24)
        target = jnp.where(inside, value, target)
        sign = jnp.where(inside & (t >= 8), -1.0, sign)
    match = lax.broadcasted_iota(jnp.int32, (256, 192), 0) == target
    choose = (jnp.where(match, 1.0, 0.0), jnp.where(match, sign, 0.0))
    wait_i()
    sums = []
    for ct in range(2):
        terms = recv_i[:, 24 * ct : 24 * ct + 24, :].reshape(192, 128)
        sums.append(
            jnp.dot(
                choose[ct], terms, precision=lax.Precision.HIGHEST, preferred_element_type=F32
            )
        )
    lane256 = lane_iota((256, 128))
    send_k[0:256, :] = jnp.where(lane256 < 64, sums[0], pltpu.roll(sums[1], 64, 1))
    send_k[256:512, :] = jnp.where(lane256 < 64, pltpu.roll(sums[0], 64, 1), sums[1])

    def chunk8(ref):
        return lambda peer: ref.at[pl.ds(pl.multiple_of(peer * 8, 8), 8), :]

    wait_k, sent_k = exchange(
        FAR, far, far_id, chunk8(send_k), chunk8(recv_k), far_sems.at[4], far_sems.at[5]
    )
    own = pl.ds(pl.multiple_of(far * 8, 8), 8)
    recv_k[own, :] = send_k[own, :]
    wait_k()
    total = recv_k[0:8, :]
    for k in range(1, FAR):
        total = total + recv_k[8 * k : 8 * k + 8, :]
    out_ref[...] = total
    for sent in (sent_a, sent_c, sent_f, sent_g, sent_i, sent_k):
        sent()


def on_device(spectra, observed, pair_table):
    table = jnp.pad(pair_table.T.astype(F32), ((0, 0), (0, 111)))
    vmem = pl.BlockSpec(memory_space=pltpu.VMEM)
    hbm = pl.BlockSpec(memory_space=pl.ANY)
    out = pl.pallas_call(
        body,
        out_shape=jax.ShapeDtypeStruct((8, 128), F32),
        in_specs=[vmem, vmem, pl.BlockSpec(memory_space=pltpu.SMEM), hbm, hbm],
        out_specs=vmem,
        scratch_shapes=[
            pltpu.VMEM((8, 48, 128), BF16),
            pltpu.VMEM((64, 8, 128), BF16),
            pltpu.VMEM((64, 8, 128), BF16),
            pltpu.VMEM((512, 128), F32),
            pltpu.VMEM((2, 1024, 128), F32),
            pltpu.VMEM((256, 1024), BF16),
            pltpu.VMEM((576, 1024), BF16),
            pltpu.VMEM((1024, 128), F32),
            pltpu.VMEM((1024, 128), BF16),
            pltpu.VMEM((1024, 128), BF16),
            pltpu.VMEM((8, 64, 256), BF16),
            pltpu.VMEM((8, 64, 256), BF16),
            pltpu.VMEM((4, 56, 512), F32),
            pltpu.VMEM((8, 48, 128), F32),
            pltpu.VMEM((8, 48, 128), F32),
            pltpu.VMEM((512, 128), F32),
            pltpu.VMEM((512, 128), F32),
            pltpu.VMEM((7, 6, 512), F32),
            pltpu.VMEM((4, 512, 512), BF16),
            pltpu.SemaphoreType.DMA((3,)),
            pltpu.SemaphoreType.DMA((6, NEAR)),
            pltpu.SemaphoreType.DMA((6, FAR)),
        ],
        compiler_params=pltpu.CompilerParams(collective_id=0, has_side_effects=True),
    )(spectra.reshape(48, F), table, pair_table, observed, lag_kernel())
    return out[:STA_DEV].reshape(STA_DEV, 2, 64)


def solution(mesh):
    torus = Mesh(mesh.devices.reshape(8, 4, 2, 4, 2), ("sta_0", "sta_1", "seg_0", "seg_1", "seg_2"))
    in_specs = (P(STA, SEG, None, None), P(STA, None, None, None), P(STA, None))
    out_specs = P(STA, None, SEG)
    return jax.shard_map(
        on_device, mesh=torus, in_specs=in_specs, out_specs=out_specs, check_vma=False
    )
```

time: 427 us -> 101 us (0.24)
  blocking collectives: 114 us -> 0 us
  waiting for transfers between devices: 95.1 us -> 0 us
  Pallas kernels: 0 us -> 86.4 us
  local copies, waits for them, and re-layouts: 72.9 us -> 3.31 us
  loops' own time: 61.8 us -> 0 us
  other arithmetic: 40.3 us -> 10.7 us
  starting transfers between devices: 24.6 us -> 0 us
  between operations: 13.8 us -> 0.05 us
    pallas_call x0 -> x1, Pallas kernels: none -> 86.4 us  [on_device(): pl.pallas_call(body, out_shape=jax.ShapeDtypeStruct((8, 128), F32), in_sp...]
    all_gather x1 -> x0, waiting for transfers between devices: 72.9 us -> none  [all_blocks(): pieces = lax.all_gather(pieces, axes[k])]
    all_to_all x3 -> x0, blocking collectives: 64.6 us -> none  [the longest x2 36 us: turned_blocks(): lax.all_to_all(pieces, axes[k], split_axis=k, concat_axis=k, tiled=True)]
    another operation x1 -> x0, loops' own time: 61.8 us -> none  [slot_cross(): return lax.map(one_slot, starts_all)]
    all_gather x1 -> x0, blocking collectives: 49 us -> none  [all_blocks(): pieces = lax.all_gather(pieces, axes[k])]
    all_to_all x2 -> x0, starting transfers between devices: 24.6 us -> none  [the longest x1 15.5 us: on_device(): owned = lax.all_to_all(flat, SEG, split_axis=0, concat_axis=2, tiled=True)]
    dynamic_slice x34 -> x0, local copies, waits for them, and re-layouts: 24.2 us -> none  [the longest x17 22.9 us: one_slot(): left = lax.dynamic_slice_in_dim(gathered, starts[0], station_count, 0)]
    all_to_all x2 -> x0, waiting for transfers between devices: 22.2 us -> none  [the longest x1 16.9 us: on_device(): lax.all_to_all(jnp.stack([common, twist], axis=1), SEG, split_axis=2, con...]
  transfers between devices with their start and end apart: 3 -> 0, of which waited for: 3 -> 0; matrix products, arithmetic and copies ran while one was open for 3% -> 0% of each run, Pallas kernels for 0% -> 0%
where the time goes in v1:
time: 101 us; the launch traced here: 100 us
  Pallas kernels  86.4 us (86%)
  other arithmetic  10.7 us (11%)
  local copies, waits for them, and re-layouts  3.31 us (3%)
    pallas_call x1, Pallas kernels, on_device(): pl.pallas_call(body, out_shape=jax.ShapeDtypeStruct((8, 128), F32), in_sp...  86.4 us
    another operation x1, other arithmetic  9.13 us

profile of v1, /device:TPU:1, one launch (start us, length us, event | category | flops | bytes accessed | tf_op | source)
XLA Modules:
  0.0 100.4 jit_solution(1843416717255811162)
XLA Ops:
  0.0 9.1 %cosine_convert_fusion = (bf16[1,2,4,2,64,512]{5,4,1,2,0,3:T(8,128)(2,1)S(1)}, bf16[1,2,4,2,64,512]{5,4,1,2,0,3:T(8,128)(2,1)S(1)}) fusion(s32[512]{0:T(512)S(1)} %iota_add_fusion, s32[2,4,2,64]{3,0,1,2:T(2,128)S(1)} %multiply_add_fusion), kind=kLoop, calls=%fused_computation.10 | loop fusion | flops 8912896 | bytes 2103296 | tf_op jit(solution)/shard_map/convert
  9.2 0.0 copy-start
  9.2 0.0 copy-start.1
  9.2 1.5 %pad_maximum_fusion = bf16[2,2,4,2,64,512]{5,4,1,2,0,3:T(8,128)(2,1)} fusion(bf16[1,2,4,2,64,512]{5,4,1,2,0,3:T(8,128)(2,1)S(1)} %get-tuple-element.6, bf16[1,2,4,2,64,512]{5,4,1,2,0,3:T(8,128)(2,1)S(1)} %get-tuple-element.5), kind=kLoop, calls=%fused_computation.8 | loop fusion | flops 1048576 | bytes 4194304 | tf_op jit(solution)/shard_map/stack | solution.py:30
  10.7 0.0 copy-done
  10.7 0.7 reshape.105.x_ref
  11.4 0.0 copy-done.1
  11.4 0.7 copy.4.pairs_ref
  12.1 0.6 pad.4.table_ref
  12.7 86.4 %shard_map.37 = f32[8,128]{1,0:T(8,128)} custom-call(bf16[48,1024]{1,0:T(8,128)(2,1)} %reshape.105.x_ref, f32[2,128]{1,0:T(2,128)} %pad.4.table_ref, s32[17,2]{1,0:T(8,128)} %copy.4.pairs_ref, f32[17,6,6,512]{3,2,1,0:T(8,128)} %observed_ref.1, bf16[4,512,512]{2,1,0:T(8,128)(2,1)} %bitcast.6), custom_call_target="tpu_custom_call" | custom-call | tf_op jit(solution)/shard_map/pallas_call | solution.py:332
  99.0 1.4 %reshape.107 = f32[6,2,64]{2,1,0:T(2,128)} reshape(f32[6,128]{1,0:T(8,128)} %bitcast.7) | data formatting | bytes 6144 | tf_op jit(solution)/shard_map/reshape | solution.py:363
  (3 shorter events, 0.0 us)
Async XLA Ops:
  9.2 1.5 %copy-start = (bf16[6,4,2,1024]{3,2,1,0:T(2,128)(2,1)S(1)}, bf16[6,4,2,1024]{3,2,1,0:T(2,128)(2,1)}, u32[]{:S(2)}) copy-start(bf16[6,4,2,1024]{3,2,1,0:T(2,128)(2,1)} %param.3) | copy-start | bytes 294916
  9.2 2.2 %copy-start.1 = (s32[17,2]{0,1:T(2,128)S(1)}, s32[17,2]{0,1:T(2,128)}, u32[]{:S(2)}) copy-start(s32[17,2]{0,1:T(2,128)} %param.5) | copy-start | bytes 412

commit v2 on v1

v2 whole, which is shorter than its diff:
```python
import math

import jax
import jax.numpy as jnp
import numpy as np
from jax import lax
from jax.experimental import pallas as pl
from jax.experimental.pallas import tpu as pltpu
from jax.sharding import Mesh
from jax.sharding import PartitionSpec as P

F = 1024
LAGS = 512
STA_DEV = 6
SEGS = 64
SEG = ("seg_0", "seg_1", "seg_2")
STA = ("sta_0", "sta_1")
SCALE = 1.0 / math.sqrt(F * SEGS)
NEAR = 8
FAR = 64
F32 = jnp.float32
BF16 = jnp.bfloat16
NT = (((1,), (1,)), ((), ()))


def lag_kernel():
    frequency = np.arange(F, dtype=np.int32)[:, None]
    offset = np.arange(LAGS, dtype=np.int32)[None, :] - LAGS // 2
    phase = np.mod(frequency * offset, 2 * F)
    angle = np.float32(math.pi / F) * phase.astype(np.float32)
    kernel = np.stack([np.cos(angle), -np.sin(angle)], axis=0)
    kernel = kernel.reshape(2, 2, 4, 2, 64, LAGS).transpose(3, 0, 2, 1, 4, 5)
    return jnp.asarray(kernel.reshape(4, 512, LAGS).astype(BF16))


def lane_maps():
    maps = np.zeros((8, 256, 128), np.float32)
    for a in range(STA_DEV):
        for b in range(STA_DEV):
            pair = STA_DEV * a + b
            for fc in range(4):
                row = 32 * a + 8 * fc + b
                if pair < 32:
                    maps[0, row, 32 * fc + pair] = 1
                    h, i, j = pair // 16, pair // 4 % 4, pair % 4
                    maps[5 + h, row, 32 * i + 8 * fc + 4 + j] = 1
                else:
                    for i in range(4):
                        maps[1 + i, row, 32 * i + 8 * fc + pair - 32] = 1
                    maps[7, row, 8 * fc + 4 + pair - 32] = 1
    return jnp.asarray(maps.astype(BF16))


def thirds(value):
    first = value.astype(BF16)
    rest = value - first.astype(F32)
    second = rest.astype(BF16)
    return first, second, (rest - second.astype(F32)).astype(BF16)


def sixths(index):
    return sum((index >= 6 * i).astype(jnp.int32) for i in range(1, 6))


def far_id(index):
    return {"seg_0": index // 32, "sta_0": (index // 4) % 8, "sta_1": index % 4}


def near_id(index):
    return {"seg_1": index // 2, "seg_2": index % 2}


def exchange(count, me, device_of, source, target, send_sems, recv_sems):
    def copy_to(peer):
        return pltpu.make_async_remote_copy(
            src_ref=source(peer),
            dst_ref=target(me),
            send_sem=send_sems.at[peer],
            recv_sem=recv_sems.at[me],
            device_id=device_of(peer),
            device_id_type=pl.DeviceIdType.MESH,
        )

    def arrival_of(peer):
        return pltpu.make_async_remote_copy(
            src_ref=source(peer),
            dst_ref=target(peer),
            send_sem=send_sems.at[peer],
            recv_sem=recv_sems.at[peer],
            device_id=device_of(peer),
            device_id_type=pl.DeviceIdType.MESH,
        )

    def each(action):
        def step(i, carry):
            if count == FAR:
                i = count - i
                j = i // 4
                dz = (j + 1) // 2 * (1 - 2 * ((j + 1) % 2))
                peer = lax.rem(me // 4 + dz + 16, 16) * 4 + lax.rem(me + i, 4)
            else:
                peer = lax.rem(me + i, count)
            action(peer)
            return carry

        lax.fori_loop(1, count, step, 0)

    each(lambda peer: copy_to(peer).start())
    return (
        lambda: each(lambda peer: arrival_of(peer).wait_recv()),
        lambda: each(lambda peer: copy_to(peer).wait_send()),
    )


def lane_iota(shape):
    return lax.broadcasted_iota(jnp.int32, shape, len(shape) - 1)


def body(
    x_hbm, pairs_hbm, observed_ref, kernel_ref, maps_ref, out_ref,
    x_raw, x_wide, x_ref, recv_a, send_b, recv_c, stage_b, stage_g, gram_m, onehot,
    stage_f, send_f, recv_f, send_g, recv_g, s_ref, send_i, recv_i, send_k, recv_k,
    obs_v, obs_rest, obs_rows, kern_v, maps_v, pairs_ref,
    local_sems, near_sems, far_sems, ring_sems,
):
    zh = lax.axis_index("seg_0")
    far = zh * 32 + lax.axis_index("sta_0") * 4 + lax.axis_index("sta_1")
    near = lax.axis_index("seg_1") * 2 + lax.axis_index("seg_2")
    seg = zh * 8 + near

    load_x = pltpu.make_async_copy(x_hbm, x_raw, local_sems.at[0])
    load_pairs = pltpu.make_async_copy(pairs_hbm, pairs_ref, local_sems.at[1])
    loads = [
        pltpu.make_async_copy(observed_ref.at[seg], obs_v, local_sems.at[2]),
        pltpu.make_async_copy(observed_ref.at[16], obs_rest, local_sems.at[3]),
        pltpu.make_async_copy(kernel_ref, kern_v, local_sems.at[4]),
        pltpu.make_async_copy(maps_ref, maps_v, local_sems.at[5]),
    ]
    barrier = pltpu.get_barrier_semaphore()

    z, y = far // 4, far % 4

    def beside(dz, dy):
        return far_id(lax.rem(z + dz + 16, 16) * 4 + lax.rem(y + dy, 4))

    def greet(semaphore, device):
        pl.semaphore_signal(
            semaphore, inc=1, device_id=device, device_id_type=pl.DeviceIdType.MESH
        )

    for i in range(1, NEAR):
        greet(barrier, near_id(lax.rem(near + i, NEAR)))
    for dy in (1, 2, 3):
        greet(barrier, beside(0, dy))
    for dz in (1, -1):
        greet(barrier, beside(dz, 0))
    load_x.start()
    load_pairs.start()
    for load in loads:
        load.start()
    load_pairs.wait()
    lane = lane_iota((1, 128))
    for end in range(2):
        row = jnp.zeros((1, 128), F32)
        for slot in range(17):
            row = jnp.where(lane == slot, pairs_ref[end, slot].astype(F32), row)
        stage_b[pl.ds(6 + end, FAR, stride=8), :] = jnp.broadcast_to(row, (FAR, 128))
    load_x.wait()
    for i in range(24):
        x_wide[2 * i : 2 * i + 2, :] = x_raw[i // 4, i % 4].astype(F32)
    x_ref[...] = x_wide[...].astype(BF16)
    pl.semaphore_wait(barrier, NEAR - 1 + 5)

    wait_a, sent_a = exchange(
        NEAR, near, near_id,
        lambda peer: x_ref.at[:, pl.ds(pl.multiple_of(peer * 128, 128), 128)],
        lambda peer: recv_a.at[peer],
        near_sems.at[0], near_sems.at[1],
    )
    recv_a[near] = x_ref[:, pl.ds(pl.multiple_of(near * 128, 128), 128)]

    for step, distance in enumerate((1, 2, 4)):
        greet(ring_sems.at[step], beside(distance, 0))
        greet(ring_sems.at[step], beside(-distance, 0))
        pl.semaphore_wait(ring_sems.at[step], 2)
    greet(ring_sems.at[3], beside(-1, 0))
    pl.semaphore_wait(ring_sems.at[3], 1)
    wait_a()

    for pair in range(3):
        rows = []
        for a in (2 * pair, 2 * pair + 1):
            for m in range(NEAR):
                rows.append(recv_a[m].astype(F32)[8 * a : 8 * a + 8])
        turned = jnp.concatenate(rows, axis=0).T
        for fi in range(2):
            stage_b[pl.ds(3 * fi + pair, FAR, stride=8), :] = turned[64 * fi : 64 * fi + 64]
    send_b[...] = stage_b[...].reshape(FAR, 8, 128).astype(BF16)
    wait_c, sent_c = exchange(
        FAR, far, far_id,
        lambda peer: send_b.at[peer], lambda peer: recv_c.at[peer],
        far_sems.at[0], far_sems.at[1],
    )
    recv_c[far] = send_b[far]
    for load in loads:
        load.wait()
    for a in range(STA_DEV):
        obs_rows[6 * a : 6 * a + 6, :] = obs_v[a]
    for j in range(4):
        pair = jnp.minimum(4 * seg + j, 35)
        obs_rows[36 + j : 37 + j, :] = obs_rest[pair // 6, pl.ds(pair % 6, 1), :]
    wait_c()
    stage_b[...] = recv_c[...].astype(F32).reshape(FAR * 8, 128)

    lane32 = lane_iota((32, 128))
    for fi in range(2):
        stations = []
        for pair in range(3):
            both = stage_b[pl.ds(3 * fi + pair, FAR, stride=8), :]
            low, high = both[0:32], both[32:64]
            stations.append(jnp.where(lane32 < 64, low, pltpu.roll(high, 64, 1)))
            stations.append(jnp.where(lane32 < 64, pltpu.roll(low, 64, 1), high))
        stations += [jnp.zeros((32, 128), F32)] * 2
        plain = jnp.concatenate(stations, axis=0)
        even = lax.rem(lane_iota((256, 128)), 2) == 0
        turned = jnp.where(even, pltpu.roll(plain, 127, 1), -pltpu.roll(plain, 1, 1))
        right = plain.astype(BF16)
        for c, left in enumerate((right, turned.astype(BF16))):
            gram = lax.dot_general(right, left, NT, preferred_element_type=F32)
            at = 256 * (2 * fi + c)
            stage_g[0, at : at + 256, :] = gram[:, 0:128]
            stage_g[1, at : at + 256, :] = gram[:, 128:256]

    for a in range(STA_DEV):
        for tile in range(8):
            kept = None
            for i in range(4):
                piece = stage_g[a // 4, pl.ds(4 * tile + i, 32, stride=32), :]
                shift = 32 * ((i - a) % 4)
                piece = pltpu.roll(piece, shift, 1) if shift else piece
                kept = piece if kept is None else jnp.where(lane32 >= 32 * i, piece, kept)
            gram_m[32 * a : 32 * a + 32, 128 * tile : 128 * tile + 128] = kept.astype(BF16)
    gram_m[192:256, :] = jnp.zeros((64, 1024), BF16)

    first = stage_b[pl.ds(6, FAR, stride=8), :]
    second = stage_b[pl.ds(7, FAR, stride=8), :]
    key = (second * 32.0 + first).astype(jnp.int32)
    row64 = lax.broadcasted_iota(jnp.int32, (FAR, 128), 0)
    main_key = jnp.where(row64 < 32, key, pltpu.roll(key, 120, 1))
    lane1024 = lane_iota((FAR, 1024))
    for m in range(NEAR + 1):
        column = key[:, 16:17] if m == NEAR else main_key[:, m : m + 1]
        hit = jnp.where(lane1024 == column, 1.0, 0.0)
        onehot[64 * m : 64 * m + 64, :] = hit.astype(BF16)
    slots = lax.dot_general(onehot[...], gram_m[...], NT, preferred_element_type=F32)
    slots = slots.astype(BF16)
    kept = jnp.dot(slots[0:512], maps_v[0], preferred_element_type=F32)
    for m in range(NEAR):
        stage_f[pl.ds(m, FAR, stride=16), :] = kept[64 * m : 64 * m + 64]
    rest = slots[512:576]
    upper = lax.broadcasted_iota(jnp.int32, (FAR, 256), 0) < 32
    rest_low = jnp.where(upper, rest, jnp.zeros_like(rest))
    rest_high = jnp.where(upper, jnp.zeros_like(rest), rest)
    for h in range(2):
        tail = jnp.dot(rest_low, maps_v[5 + h], preferred_element_type=F32)
        if h == 0:
            tail = tail + jnp.dot(rest_high, maps_v[7], preferred_element_type=F32)
        for i in range(4):
            at = 64 * (4 * h + i)
            tail = tail + jnp.dot(
                slots[at : at + 64], maps_v[1 + i], preferred_element_type=F32
            )
        stage_f[pl.ds(8 + h, FAR, stride=16), :] = tail
    send_f[...] = stage_f[...].astype(BF16)

    def chunk16(ref):
        return lambda peer: ref.at[pl.ds(pl.multiple_of(peer * 16, 16), 10), :]

    wait_f, sent_f = exchange(
        FAR, far, far_id, chunk16(send_f), chunk16(recv_f), far_sems.at[2], far_sems.at[3]
    )
    own = pl.ds(pl.multiple_of(far * 16, 16), 16)
    recv_f[own, :] = send_f[own, :]
    wait_f()
    stage_f[...] = recv_f[...].astype(F32)
    lane16 = lane_iota((16, 128))
    tails = [stage_f[pl.ds(8 + h, FAR, stride=16), :] for h in range(2)]
    for m in range(NEAR):
        send_g[m, 0:64, :] = stage_f[pl.ds(m, FAR, stride=16), :].astype(BF16)
        packed = None
        for i in range(4):
            piece = tails[m // 4][16 * i : 16 * i + 16]
            shift = 32 * ((i - m) % 4)
            piece = pltpu.roll(piece, shift, 1) if shift else piece
            packed = piece if packed is None else jnp.where(lane16 >= 32 * i, piece, packed)
        send_g[m, 64:80, :] = packed.astype(BF16)
    wait_g, sent_g = exchange(
        NEAR, near, near_id,
        lambda peer: send_g.at[peer], lambda peer: recv_g.at[peer],
        near_sems.at[2], near_sems.at[3],
    )
    recv_g[near] = send_g[near]
    wait_g()

    tail_rows = []
    for m in range(NEAR):
        blocks = recv_g[m, 64:80, :].astype(F32)
        for i in range(4):
            shift = 32 * ((m - i) % 4)
            tail_rows.append(pltpu.roll(blocks, shift, 1) if shift else blocks)
    lane128 = lane_iota((128, 128))
    tail = None
    for xt in range(4):
        both = jnp.concatenate(tail_rows[4 * xt : 4 * xt + 4] + tail_rows[4 * xt + 16 : 4 * xt + 20])
        tail = both if tail is None else jnp.where(lane128 >= 32 * xt, both, tail)
    tail = tail.T
    for xt in range(4):
        lanes = slice(128 * xt, 128 * xt + 128)
        square = jnp.concatenate(
            [recv_g[xt, 0:64, :].astype(F32), recv_g[4 + xt, 0:64, :].astype(F32)], axis=0
        ).T
        for fc in range(4):
            s_ref[fc, 0:32, lanes] = square[32 * fc : 32 * fc + 32]
            s_ref[fc, 32:40, lanes] = tail[32 * xt + 8 * fc : 32 * xt + 8 * fc + 8]
    lags = jnp.zeros((40, LAGS), F32)
    for fc in range(4):
        lags = lags + jnp.dot(s_ref[fc].astype(BF16), kern_v[fc], preferred_element_type=F32)

    def floor_of(slot):
        p, q = pairs_ref[0, slot], pairs_ref[1, slot]
        return jnp.where(p < 0, 99, jnp.where(p != q, -99, 0))

    row = lax.broadcasted_iota(jnp.int32, (40, LAGS), 0)
    pair = jnp.where(row < 36, row, jnp.minimum(row - 36 + 4 * seg, 35))
    floor = jnp.where(row < 36, floor_of(seg), jnp.where(seg < 9, floor_of(16), 99))
    keep = pair - 7 * sixths(pair) > floor
    value = jnp.tanh(SCALE * lags - obs_rows[...])
    residual = jnp.where(keep, value, 0.0).astype(BF16)

    to = lax.broadcasted_iota(jnp.int32, (16, 40), 0)
    of = lane_iota((16, 40))
    first_of = sixths(of)
    main = of < 36
    picked = (to < 6) & main & (first_of == to)
    picked = picked | ((to >= 6) & (to < 12) & main & (of - 6 * first_of == to - 6))
    picked = picked | ((of >= 36) & (of - 36 == to - 12))
    picked = jnp.where(picked, 1.0, 0.0).astype(BF16)
    for fi in range(2):
        gamma = [
            SCALE * lax.dot_general(residual, kern_v[2 * fi + c], NT, preferred_element_type=F32)
            for c in range(2)
        ]
        s0, s1 = s_ref[2 * fi], s_ref[2 * fi + 1]
        common = gamma[0] * s0 + gamma[1] * s1
        twist = gamma[1] * s0 - gamma[0] * s1
        for ct, term in enumerate((common, twist)):
            block = sum(
                jnp.dot(picked, third, preferred_element_type=F32) for third in thirds(term)
            )
            for xt in range(4):
                send_i[2 * xt + fi, 16 * ct : 16 * ct + 16, :] = block[:, 128 * xt : 128 * xt + 128]
    wait_i, sent_i = exchange(
        NEAR, near, near_id,
        lambda peer: send_i.at[peer], lambda peer: recv_i.at[peer],
        near_sems.at[4], near_sems.at[5],
    )
    recv_i[near] = send_i[near]

    lane = lane_iota((1, 128))
    source = lax.shift_right_logical(lane, 4)
    t = lane - 16 * source
    p_main = jnp.full((1, 128), -1, jnp.int32)
    q_main = p_main
    for m in range(NEAR):
        p_main = jnp.where(source == m, pairs_ref[0, zh * 8 + m], p_main)
        q_main = jnp.where(source == m, pairs_ref[1, zh * 8 + m], q_main)
    pair = jnp.clip(32 * zh + 4 * source + t - 12, 0, 35)
    valid = 32 * zh + 4 * source + t - 12 < 36
    a_rest = sixths(pair)
    plus = jnp.where(
        t < 6, 8 * p_main + t,
        jnp.where((t >= 12) & valid, 8 * pairs_ref[0, 16] + a_rest, -1),
    )
    minus = jnp.where(
        (t >= 6) & (t < 12), 8 * q_main + t - 6,
        jnp.where((t >= 12) & valid, 8 * pairs_ref[1, 16] + pair - 6 * a_rest, -1),
    )
    station = lax.broadcasted_iota(jnp.int32, (256, 128), 0)
    plus = jnp.where(station == plus, 1.0, 0.0)
    minus = jnp.where(station == minus, 1.0, 0.0)
    choose = ((plus + minus).astype(BF16), (plus - minus).astype(BF16))
    wait_i()
    sums = []
    for ct in range(2):
        terms = recv_i[:, 16 * ct : 16 * ct + 16, :].reshape(128, 128)
        sums.append(
            sum(jnp.dot(choose[ct], third, preferred_element_type=F32) for third in thirds(terms))
        )
    lane256 = lane_iota((256, 128))
    send_k[0:256, :] = jnp.where(lane256 < 64, sums[0], pltpu.roll(sums[1], 64, 1))
    send_k[256:512, :] = jnp.where(lane256 < 64, pltpu.roll(sums[0], 64, 1), sums[1])

    def chunk8(ref):
        return lambda peer: ref.at[pl.ds(pl.multiple_of(peer * 8, 8), STA_DEV), :]

    wait_k, sent_k = exchange(
        FAR, far, far_id, chunk8(send_k), chunk8(recv_k), far_sems.at[4], far_sems.at[5]
    )
    own = pl.ds(pl.multiple_of(far * 8, 8), 8)
    recv_k[own, :] = send_k[own, :]
    wait_k()
    total = recv_k[0:8, :]
    for k in range(1, FAR):
        total = total + recv_k[8 * k : 8 * k + 8, :]
    out_ref[:, 0, :] = total[0:STA_DEV, 0:64]
    out_ref[:, 1, :] = total[0:STA_DEV, 64:128]
    for sent in (sent_a, sent_c, sent_f, sent_g, sent_i, sent_k):
        sent()


def on_device(spectra, observed, pair_table):
    vmem = pl.BlockSpec(memory_space=pltpu.VMEM)
    hbm = pl.BlockSpec(memory_space=pl.ANY)
    return pl.pallas_call(
        body,
        out_shape=jax.ShapeDtypeStruct((STA_DEV, 2, 64), F32),
        in_specs=[hbm] * 5,
        out_specs=vmem,
        scratch_shapes=[
            pltpu.VMEM((6, 4, 2, 1024), BF16),
            pltpu.VMEM((48, 1024), F32),
            pltpu.VMEM((48, 1024), BF16),
            pltpu.VMEM((8, 48, 128), BF16),
            pltpu.VMEM((64, 8, 128), BF16),
            pltpu.VMEM((64, 8, 128), BF16),
            pltpu.VMEM((512, 128), F32),
            pltpu.VMEM((2, 1024, 128), F32),
            pltpu.VMEM((256, 1024), BF16),
            pltpu.VMEM((576, 1024), BF16),
            pltpu.VMEM((1024, 128), F32),
            pltpu.VMEM((1024, 128), BF16),
            pltpu.VMEM((1024, 128), BF16),
            pltpu.VMEM((8, 80, 128), BF16),
            pltpu.VMEM((8, 80, 128), BF16),
            pltpu.VMEM((4, 40, 512), F32),
            pltpu.VMEM((8, 32, 128), F32),
            pltpu.VMEM((8, 32, 128), F32),
            pltpu.VMEM((512, 128), F32),
            pltpu.VMEM((512, 128), F32),
            pltpu.VMEM((6, 6, 512), F32),
            pltpu.VMEM((6, 6, 512), F32),
            pltpu.VMEM((40, 512), F32),
            pltpu.VMEM((4, 512, 512), BF16),
            pltpu.VMEM((8, 256, 128), BF16),
            pltpu.SMEM((2, 17), jnp.int32),
            pltpu.SemaphoreType.DMA((6,)),
            pltpu.SemaphoreType.DMA((6, NEAR)),
            pltpu.SemaphoreType.DMA((6, FAR)),
            pltpu.SemaphoreType.REGULAR((4,)),
        ],
        compiler_params=pltpu.CompilerParams(collective_id=0, has_side_effects=True),
    )(spectra, pair_table.T, observed, lag_kernel(), lane_maps())


def solution(mesh):
    torus = Mesh(mesh.devices.reshape(8, 4, 2, 4, 2), ("sta_0", "sta_1", "seg_0", "seg_1", "seg_2"))
    in_specs = (P(STA, SEG, None, None), P(STA, None, None, None), P(STA, None))
    out_specs = P(STA, None, SEG)
    return jax.shard_map(
        on_device, mesh=torus, in_specs=in_specs, out_specs=out_specs, check_vma=False
    )
```

time: 101 us -> 79.9 us (0.79)
  other arithmetic: 10.7 us -> 0 us
  Pallas kernels: 86.4 us -> 78.4 us
  local copies, waits for them, and re-layouts: 3.31 us -> 1.29 us
    another operation x2 -> x0, other arithmetic: 10.6 us -> none
    pallas_call x1, Pallas kernels: 86.4 us -> 78.4 us  [on_device(): pl.pallas_call(body, out_shape=jax.ShapeDtypeStruct((STA_DEV, 2, 64), F32...]
    reshape x2 -> x0, local copies, waits for them, and re-layouts: 2.04 us -> none  [the longest x1 1.35 us: on_device(): return out[:STA_DEV].reshape(STA_DEV, 2, 64)]
where the time goes in v2:
time: 79.9 us; the launch traced here: 79.7 us
  Pallas kernels  78.4 us (98%)
  local copies, waits for them, and re-layouts  1.29 us (2%)
    pallas_call x1, Pallas kernels, on_device(): pl.pallas_call(body, out_shape=jax.ShapeDtypeStruct((STA_DEV, 2, 64), F32...  78.4 us

profile of v2, /device:TPU:1, one launch (start us, length us, event | category | flops | bytes accessed | tf_op | source)
XLA Modules:
  0.0 79.7 jit_solution(14455290180599253812)
XLA Ops:
  0.0 78.4 %shard_map.55 = f32[6,2,64]{2,1,0:T(2,128)} custom-call(bf16[6,4,2,1024]{3,2,1,0:T(2,128)(2,1)} %x_hbm.1, s32[2,17]{1,0:T(2,128)} %bitcast.1, f32[17,6,6,512]{3,2,1,0:T(8,128)} %observed_ref.1, bf16[4,512,512]{2,1,0:T(8,128)(2,1)} %constant.4.clone.kernel_ref, bf16[8,256,128]{2,1,0:T(8,128)(2,1)} %constant.5.clone.maps_ref), custom_call_target="tpu_custom_call" | custom-call | tf_op jit(solution)/shard_map/pallas_call | solution.py:424
  78.4 1.3 %copy.7 = f32[6,2,64]{2,1,0:T(2,128)} copy(f32[6,2,64]{2,1,0:T(2,128)} %shard_map.55) | data formatting | bytes 6144

commit v3 on v2

--- a/solution.py
+++ b/solution.py
@@ -70,46 +70,49 @@
     return {"seg_1": index // 2, "seg_2": index % 2}
 
 
-def exchange(count, me, device_of, source, target, send_sems, recv_sems):
-    def copy_to(peer):
-        return pltpu.make_async_remote_copy(
-            src_ref=source(peer),
-            dst_ref=target(me),
-            send_sem=send_sems.at[peer],
-            recv_sem=recv_sems.at[me],
-            device_id=device_of(peer),
-            device_id_type=pl.DeviceIdType.MESH,
-        )
-
-    def arrival_of(peer):
-        return pltpu.make_async_remote_copy(
-            src_ref=source(peer),
-            dst_ref=target(peer),
-            send_sem=send_sems.at[peer],
-            recv_sem=recv_sems.at[peer],
-            device_id=device_of(peer),
-            device_id_type=pl.DeviceIdType.MESH,
-        )
-
-    def each(action):
-        def step(i, carry):
-            if count == FAR:
-                i = count - i
-                j = i // 4
-                dz = (j + 1) // 2 * (1 - 2 * ((j + 1) % 2))
-                peer = lax.rem(me // 4 + dz + 16, 16) * 4 + lax.rem(me + i, 4)
-            else:
-                peer = lax.rem(me + i, count)
-            action(peer)
-            return carry
-
-        lax.fori_loop(1, count, step, 0)
-
-    each(lambda peer: copy_to(peer).start())
-    return (
-        lambda: each(lambda peer: arrival_of(peer).wait_recv()),
-        lambda: each(lambda peer: copy_to(peer).wait_send()),
-    )
+def landed(ref, semaphore):
+    pltpu.make_async_copy(ref, ref, semaphore).wait()
+
+
+def send(source, target, semaphores, at, device):
+    pltpu.make_async_remote_copy(
+        src_ref=source,
+        dst_ref=target,
+        send_sem=semaphores.at[at],
+        recv_sem=semaphores.at[at + 1],
+        device_id=device,
+        device_id_type=pl.DeviceIdType.MESH,
+    ).start()
+
+
+def send_near(me, source, target, semaphores, at):
+    for i in range(1, NEAR):
+        peer = lax.rem(me + i, NEAR)
+        send(source(peer), target(me), semaphores, at, near_id(peer))
+
+
+def send_far(me, source, target, semaphores, at, farthest_first):
+    z, y = me // 4, lax.rem(me, 4)
+    ys = [lax.rem(y + dy, 4) for dy in range(4)]
+
+    def to_chip(peer_z, dys):
+        zh, zl = peer_z // 8, lax.rem(peer_z, 8)
+        for dy in dys:
+            peer = peer_z * 4 + ys[dy]
+            device = {"seg_0": zh, "sta_0": zl, "sta_1": ys[dy]}
+            send(source(peer), target(me), semaphores, at, device)
+
+    def step(j, carry):
+        if farthest_first:
+            j = 16 - j
+            dz = (j + 1) // 2 * (1 - 2 * lax.rem(j + 1, 2))
+            to_chip(lax.rem(z + dz + 16, 16), range(4))
+        else:
+            to_chip(lax.rem(z + j, 16), range(4))
+        return carry
+
+    lax.fori_loop(1, 16, step, 0)
+    to_chip(z, (1, 2, 3))
 
 
 def lane_iota(shape):
@@ -121,7 +124,7 @@
     x_raw, x_wide, x_ref, recv_a, send_b, recv_c, stage_b, stage_g, gram_m, onehot,
     stage_f, send_f, recv_f, send_g, recv_g, s_ref, send_i, recv_i, send_k, recv_k,
     obs_v, obs_rest, obs_rows, kern_v, maps_v, pairs_ref,
-    local_sems, near_sems, far_sems, ring_sems,
+    local_sems, sems, ring_sems,
 ):
     zh = lax.axis_index("seg_0")
     far = zh * 32 + lax.axis_index("sta_0") * 4 + lax.axis_index("sta_1")
@@ -171,11 +174,11 @@
     x_ref[...] = x_wide[...].astype(BF16)
     pl.semaphore_wait(barrier, NEAR - 1 + 5)
 
-    wait_a, sent_a = exchange(
-        NEAR, near, near_id,
+    send_near(
+        near,
         lambda peer: x_ref.at[:, pl.ds(pl.multiple_of(peer * 128, 128), 128)],
         lambda peer: recv_a.at[peer],
-        near_sems.at[0], near_sems.at[1],
+        sems, 0,
     )
     recv_a[near] = x_ref[:, pl.ds(pl.multiple_of(near * 128, 128), 128)]
 
@@ -185,7 +188,7 @@
         pl.semaphore_wait(ring_sems.at[step], 2)
     greet(ring_sems.at[3], beside(-1, 0))
     pl.semaphore_wait(ring_sems.at[3], 1)
-    wait_a()
+    landed(recv_a.at[pl.ds(0, NEAR - 1)], sems.at[1])
 
     for pair in range(3):
         rows = []
@@ -196,11 +199,7 @@
         for fi in range(2):
             stage_b[pl.ds(3 * fi + pair, FAR, stride=8), :] = turned[64 * fi : 64 * fi + 64]
     send_b[...] = stage_b[...].reshape(FAR, 8, 128).astype(BF16)
-    wait_c, sent_c = exchange(
-        FAR, far, far_id,
-        lambda peer: send_b.at[peer], lambda peer: recv_c.at[peer],
-        far_sems.at[0], far_sems.at[1],
-    )
+    send_far(far, lambda peer: send_b.at[peer], lambda peer: recv_c.at[peer], sems, 2, False)
     recv_c[far] = send_b[far]
     for load in loads:
         load.wait()
@@ -209,7 +208,8 @@
     for j in range(4):
         pair = jnp.minimum(4 * seg + j, 35)
         obs_rows[36 + j : 37 + j, :] = obs_rest[pair // 6, pl.ds(pair % 6, 1), :]
-    wait_c()
+    landed(recv_a.at[pl.ds(0, NEAR - 1)], sems.at[0])
+    landed(recv_c.at[pl.ds(0, FAR - 1)], sems.at[3])
     stage_b[...] = recv_c[...].astype(F32).reshape(FAR * 8, 128)
 
     lane32 = lane_iota((32, 128))
@@ -276,12 +276,11 @@
     def chunk16(ref):
         return lambda peer: ref.at[pl.ds(pl.multiple_of(peer * 16, 16), 10), :]
 
-    wait_f, sent_f = exchange(
-        FAR, far, far_id, chunk16(send_f), chunk16(recv_f), far_sems.at[2], far_sems.at[3]
-    )
+    send_far(far, chunk16(send_f), chunk16(recv_f), sems, 4, True)
     own = pl.ds(pl.multiple_of(far * 16, 16), 16)
     recv_f[own, :] = send_f[own, :]
-    wait_f()
+    landed(send_b.at[pl.ds(0, FAR - 1)], sems.at[2])
+    landed(recv_f.at[pl.ds(0, 10 * (FAR - 1))], sems.at[5])
     stage_f[...] = recv_f[...].astype(F32)
     lane16 = lane_iota((16, 128))
     tails = [stage_f[pl.ds(8 + h, FAR, stride=16), :] for h in range(2)]
@@ -294,13 +293,10 @@
             piece = pltpu.roll(piece, shift, 1) if shift else piece
             packed = piece if packed is None else jnp.where(lane16 >= 32 * i, piece, packed)
         send_g[m, 64:80, :] = packed.astype(BF16)
-    wait_g, sent_g = exchange(
-        NEAR, near, near_id,
-        lambda peer: send_g.at[peer], lambda peer: recv_g.at[peer],
-        near_sems.at[2], near_sems.at[3],
-    )
+    send_near(near, lambda peer: send_g.at[peer], lambda peer: recv_g.at[peer], sems, 6)
     recv_g[near] = send_g[near]
-    wait_g()
+    landed(send_f.at[pl.ds(0, 10 * (FAR - 1))], sems.at[4])
+    landed(recv_g.at[pl.ds(0, NEAR - 1)], sems.at[7])
 
     tail_rows = []
     for m in range(NEAR):
@@ -359,11 +355,7 @@
             )
             for xt in range(4):
                 send_i[2 * xt + fi, 16 * ct : 16 * ct + 16, :] = block[:, 128 * xt : 128 * xt + 128]
-    wait_i, sent_i = exchange(
-        NEAR, near, near_id,
-        lambda peer: send_i.at[peer], lambda peer: recv_i.at[peer],
-        near_sems.at[4], near_sems.at[5],
-    )
+    send_near(near, lambda peer: send_i.at[peer], lambda peer: recv_i.at[peer], sems, 8)
     recv_i[near] = send_i[near]
 
     lane = lane_iota((1, 128))
@@ -389,7 +381,8 @@
     plus = jnp.where(station == plus, 1.0, 0.0)
     minus = jnp.where(station == minus, 1.0, 0.0)
     choose = ((plus + minus).astype(BF16), (plus - minus).astype(BF16))
-    wait_i()
+    landed(send_g.at[pl.ds(0, NEAR - 1)], sems.at[6])
+    landed(recv_i.at[pl.ds(0, NEAR - 1)], sems.at[9])
     sums = []
     for ct in range(2):
         terms = recv_i[:, 16 * ct : 16 * ct + 16, :].reshape(128, 128)
@@ -403,19 +396,17 @@
     def chunk8(ref):
         return lambda peer: ref.at[pl.ds(pl.multiple_of(peer * 8, 8), STA_DEV), :]
 
-    wait_k, sent_k = exchange(
-        FAR, far, far_id, chunk8(send_k), chunk8(recv_k), far_sems.at[4], far_sems.at[5]
-    )
+    send_far(far, chunk8(send_k), chunk8(recv_k), sems, 10, False)
     own = pl.ds(pl.multiple_of(far * 8, 8), 8)
     recv_k[own, :] = send_k[own, :]
-    wait_k()
+    landed(send_i.at[pl.ds(0, NEAR - 1)], sems.at[8])
+    landed(recv_k.at[pl.ds(0, STA_DEV * (FAR - 1))], sems.at[11])
     total = recv_k[0:8, :]
     for k in range(1, FAR):
         total = total + recv_k[8 * k : 8 * k + 8, :]
     out_ref[:, 0, :] = total[0:STA_DEV, 0:64]
     out_ref[:, 1, :] = total[0:STA_DEV, 64:128]
-    for sent in (sent_a, sent_c, sent_f, sent_g, sent_i, sent_k):
-        sent()
+    landed(send_k.at[pl.ds(0, STA_DEV * (FAR - 1))], sems.at[10])
 
 
 def on_device(spectra, observed, pair_table):
@@ -454,8 +445,7 @@
             pltpu.VMEM((8, 256, 128), BF16),
             pltpu.SMEM((2, 17), jnp.int32),
             pltpu.SemaphoreType.DMA((6,)),
-            pltpu.SemaphoreType.DMA((6, NEAR)),
-            pltpu.SemaphoreType.DMA((6, FAR)),
+            pltpu.SemaphoreType.DMA((12,)),
             pltpu.SemaphoreType.REGULAR((4,)),
         ],
         compiler_params=pltpu.CompilerParams(collective_id=0, has_side_effects=True),

time: 79.9 us -> 69.6 us (0.87)
  Pallas kernels: 78.4 us -> 68.1 us
    pallas_call x1, Pallas kernels: 78.4 us -> 68.1 us  [on_device(): pl.pallas_call(body, out_shape=jax.ShapeDtypeStruct((STA_DEV, 2, 64), F32...]
where the time goes in v3:
time: 69.6 us; the launch traced here: 69.4 us
  Pallas kernels  68.1 us (98%)
  local copies, waits for them, and re-layouts  1.29 us (2%)
    pallas_call x1, Pallas kernels, on_device(): pl.pallas_call(body, out_shape=jax.ShapeDtypeStruct((STA_DEV, 2, 64), F32...  68.1 us

profile of v3, /device:TPU:1, one launch (start us, length us, event | category | flops | bytes accessed | tf_op | source)
XLA Modules:
  0.0 69.4 jit_solution(12223461349015061902)
XLA Ops:
  0.0 68.1 %shard_map.55 = f32[6,2,64]{2,1,0:T(2,128)} custom-call(bf16[6,4,2,1024]{3,2,1,0:T(2,128)(2,1)} %x_hbm.1, s32[2,17]{1,0:T(2,128)} %bitcast.1, f32[17,6,6,512]{3,2,1,0:T(8,128)} %observed_ref.1, bf16[4,512,512]{2,1,0:T(8,128)(2,1)} %constant.4.clone.kernel_ref, bf16[8,256,128]{2,1,0:T(8,128)(2,1)} %constant.5.clone.maps_ref), custom_call_target="tpu_custom_call" | custom-call | tf_op jit(solution)/shard_map/pallas_call | solution.py:415
  68.1 1.3 %copy.7 = f32[6,2,64]{2,1,0:T(2,128)} copy(f32[6,2,64]{2,1,0:T(2,128)} %shard_map.55) | data formatting | bytes 6144

commit v4 on v3

--- a/solution.py
+++ b/solution.py
@@ -86,8 +86,9 @@
 
 
 def send_near(me, source, target, semaphores, at):
-    for i in range(1, NEAR):
-        peer = lax.rem(me + i, NEAR)
+    x, core = me // 2, lax.rem(me, 2)
+    for dx, change in ((2, 1), (2, 0), (1, 1), (3, 1), (1, 0), (3, 0), (0, 1)):
+        peer = lax.rem(x + dx, 4) * 2 + (1 - core if change else core)
         send(source(peer), target(me), semaphores, at, near_id(peer))
 
 
@@ -106,13 +107,13 @@
         if farthest_first:
             j = 16 - j
             dz = (j + 1) // 2 * (1 - 2 * lax.rem(j + 1, 2))
-            to_chip(lax.rem(z + dz + 16, 16), range(4))
+            to_chip(lax.rem(z + dz + 16, 16), (2, 1, 3, 0))
         else:
             to_chip(lax.rem(z + j, 16), range(4))
         return carry
 
     lax.fori_loop(1, 16, step, 0)
-    to_chip(z, (1, 2, 3))
+    to_chip(z, (2, 1, 3))
 
 
 def lane_iota(shape):
@@ -199,7 +200,7 @@
         for fi in range(2):
             stage_b[pl.ds(3 * fi + pair, FAR, stride=8), :] = turned[64 * fi : 64 * fi + 64]
     send_b[...] = stage_b[...].reshape(FAR, 8, 128).astype(BF16)
-    send_far(far, lambda peer: send_b.at[peer], lambda peer: recv_c.at[peer], sems, 2, False)
+    send_far(far, lambda peer: send_b.at[peer], lambda peer: recv_c.at[peer], sems, 2, True)
     recv_c[far] = send_b[far]
     for load in loads:
         load.wait()
@@ -396,7 +397,7 @@
     def chunk8(ref):
         return lambda peer: ref.at[pl.ds(pl.multiple_of(peer * 8, 8), STA_DEV), :]
 
-    send_far(far, chunk8(send_k), chunk8(recv_k), sems, 10, False)
+    send_far(far, chunk8(send_k), chunk8(recv_k), sems, 10, True)
     own = pl.ds(pl.multiple_of(far * 8, 8), 8)
     recv_k[own, :] = send_k[own, :]
     landed(send_i.at[pl.ds(0, NEAR - 1)], sems.at[8])
@@ -414,7 +415,7 @@
     hbm = pl.BlockSpec(memory_space=pl.ANY)
     return pl.pallas_call(
         body,
-        out_shape=jax.ShapeDtypeStruct((STA_DEV, 2, 64), F32),
+        out_shape=pltpu.VMEM((STA_DEV, 2, 64), F32),
         in_specs=[hbm] * 5,
         out_specs=vmem,
         scratch_shapes=[

time: 69.6 us -> 65.1 us (0.935)
  Pallas kernels: 68.1 us -> 64.3 us
    pallas_call x1, Pallas kernels: 68.1 us -> 64.3 us  [on_device(): pl.pallas_call(body, out_shape=pltpu.VMEM((STA_DEV, 2, 64), F32), in_spec...]
where the time goes in v4:
time: 65.1 us; the launch traced here: 64.9 us
  Pallas kernels  64.3 us (99%)
    pallas_call x1, Pallas kernels, on_device(): pl.pallas_call(body, out_shape=pltpu.VMEM((STA_DEV, 2, 64), F32), in_spec...  64.3 us

profile of v4, /device:TPU:1, one launch (start us, length us, event | category | flops | bytes accessed | tf_op | source)
XLA Modules:
  0.0 64.9 jit_solution(16940167036302251047)
XLA Ops:
  0.0 64.3 %shard_map.55 = f32[6,2,64]{2,1,0:T(2,128)S(1)} custom-call(bf16[6,4,2,1024]{3,2,1,0:T(2,128)(2,1)} %x_hbm.1, s32[2,17]{1,0:T(2,128)} %bitcast.1, f32[17,6,6,512]{3,2,1,0:T(8,128)} %observed_ref.1, bf16[4,512,512]{2,1,0:T(8,128)(2,1)} %constant.4.clone.kernel_ref, bf16[8,256,128]{2,1,0:T(8,128)(2,1)} %constant.5.clone.maps_ref), custom_call_target="tpu_custom_call" | custom-call | tf_op jit(solution)/shard_map/pallas_call | solution.py:416
  64.3 0.6 copy.7

commit v5 on v4

--- a/solution.py
+++ b/solution.py
@@ -18,6 +18,7 @@
 SCALE = 1.0 / math.sqrt(F * SEGS)
 NEAR = 8
 FAR = 64
+PITCH = 40
 F32 = jnp.float32
 BF16 = jnp.bfloat16
 NT = (((1,), (1,)), ((), ()))
@@ -228,19 +229,23 @@
         right = plain.astype(BF16)
         for c, left in enumerate((right, turned.astype(BF16))):
             gram = lax.dot_general(right, left, NT, preferred_element_type=F32)
-            at = 256 * (2 * fi + c)
-            stage_g[0, at : at + 256, :] = gram[:, 0:128]
-            stage_g[1, at : at + 256, :] = gram[:, 128:256]
-
-    for a in range(STA_DEV):
-        for tile in range(8):
-            kept = None
-            for i in range(4):
-                piece = stage_g[a // 4, pl.ds(4 * tile + i, 32, stride=32), :]
-                shift = 32 * ((i - a) % 4)
-                piece = pltpu.roll(piece, shift, 1) if shift else piece
-                kept = piece if kept is None else jnp.where(lane32 >= 32 * i, piece, kept)
-            gram_m[32 * a : 32 * a + 32, 128 * tile : 128 * tile + 128] = kept.astype(BF16)
+            for i in range(8):
+                at = PITCH * (8 * (2 * fi + c) + i)
+                stage_g[0, at : at + 32, :] = gram[32 * i : 32 * i + 32, 0:128]
+                stage_g[1, at : at + 32, :] = gram[32 * i : 32 * i + 32, 128:256]
+
+    for tile in range(8):
+        for half in range(2):
+            pieces = [
+                stage_g[half, pl.ds(4 * tile + i, 32, stride=PITCH), :] for i in range(4)
+            ]
+            for a in range(4 * half, min(4 * half + 4, STA_DEV)):
+                kept = None
+                for i, piece in enumerate(pieces):
+                    shift = 32 * ((i - a) % 4)
+                    piece = pltpu.roll(piece, shift, 1) if shift else piece
+                    kept = piece if kept is None else jnp.where(lane32 >= 32 * i, piece, kept)
+                gram_m[32 * a : 32 * a + 32, 128 * tile : 128 * tile + 128] = kept.astype(BF16)
     gram_m[192:256, :] = jnp.zeros((64, 1024), BF16)
 
     first = stage_b[pl.ds(6, FAR, stride=8), :]
@@ -426,7 +431,7 @@
             pltpu.VMEM((64, 8, 128), BF16),
             pltpu.VMEM((64, 8, 128), BF16),
             pltpu.VMEM((512, 128), F32),
-            pltpu.VMEM((2, 1024, 128), F32),
+            pltpu.VMEM((2, 32 * PITCH, 128), F32),
             pltpu.VMEM((256, 1024), BF16),
             pltpu.VMEM((576, 1024), BF16),
             pltpu.VMEM((1024, 128), F32),

time: 65.1 us -> 64.3 us (0.988)
  Pallas kernels: 64.3 us -> 63.6 us
    pallas_call x1, Pallas kernels: 64.3 us -> 63.6 us  [on_device(): pl.pallas_call(body, out_shape=pltpu.VMEM((STA_DEV, 2, 64), F32), in_spec...]
where the time goes in v5:
time: 64.3 us; the launch traced here: 64.2 us
  Pallas kernels  63.6 us (99%)
    pallas_call x1, Pallas kernels, on_device(): pl.pallas_call(body, out_shape=pltpu.VMEM((STA_DEV, 2, 64), F32), in_spec...  63.6 us

profile of v5, /device:TPU:1, one launch (start us, length us, event | category | flops | bytes accessed | tf_op | source)
XLA Modules:
  0.0 64.2 jit_solution(12794517538236177160)
XLA Ops:
  0.0 63.6 %shard_map.55 = f32[6,2,64]{2,1,0:T(2,128)S(1)} custom-call(bf16[6,4,2,1024]{3,2,1,0:T(2,128)(2,1)} %x_hbm.1, s32[2,17]{1,0:T(2,128)} %bitcast.1, f32[17,6,6,512]{3,2,1,0:T(8,128)} %observed_ref.1, bf16[4,512,512]{2,1,0:T(8,128)(2,1)} %constant.4.clone.kernel_ref, bf16[8,256,128]{2,1,0:T(8,128)(2,1)} %constant.5.clone.maps_ref), custom_call_target="tpu_custom_call" | custom-call | tf_op jit(solution)/shard_map/pallas_call | solution.py:421
  63.6 0.6 copy.7

commit v6 on v5

--- a/solution.py
+++ b/solution.py
@@ -153,16 +153,39 @@
             semaphore, inc=1, device_id=device, device_id_type=pl.DeviceIdType.MESH
         )
 
+    load_x.start()
     for i in range(1, NEAR):
         greet(barrier, near_id(lax.rem(near + i, NEAR)))
     for dy in (1, 2, 3):
         greet(barrier, beside(0, dy))
     for dz in (1, -1):
         greet(barrier, beside(dz, 0))
-    load_x.start()
     load_pairs.start()
     for load in loads:
         load.start()
+    pl.semaphore_wait(barrier, NEAR - 1 + 5)
+    for dz in (1, -1):
+        greet(ring_sems.at[0], beside(dz, 0))
+    load_x.wait()
+    for i in range(24):
+        x_wide[2 * i : 2 * i + 2, :] = x_raw[i // 4, i % 4].astype(F32)
+    x_ref[...] = x_wide[...].astype(BF16)
+
+    send_near(
+        near,
+        lambda peer: x_ref.at[:, pl.ds(pl.multiple_of(peer * 128, 128), 128)],
+        lambda peer: recv_a.at[peer],
+        sems, 0,
+    )
+    recv_a[near] = x_ref[:, pl.ds(pl.multiple_of(near * 128, 128), 128)]
+
+    for step, distance in enumerate((1, 2, 4)):
+        if step > 0:
+            greet(ring_sems.at[step], beside(distance, 0))
+            greet(ring_sems.at[step], beside(-distance, 0))
+        pl.semaphore_wait(ring_sems.at[step], 2)
+    greet(ring_sems.at[3], beside(-1, 0))
+    pl.semaphore_wait(ring_sems.at[3], 1)
     load_pairs.wait()
     lane = lane_iota((1, 128))
     for end in range(2):
@@ -170,26 +193,6 @@
         for slot in range(17):
             row = jnp.where(lane == slot, pairs_ref[end, slot].astype(F32), row)
         stage_b[pl.ds(6 + end, FAR, stride=8), :] = jnp.broadcast_to(row, (FAR, 128))
-    load_x.wait()
-    for i in range(24):
-        x_wide[2 * i : 2 * i + 2, :] = x_raw[i // 4, i % 4].astype(F32)
-    x_ref[...] = x_wide[...].astype(BF16)
-    pl.semaphore_wait(barrier, NEAR - 1 + 5)
-
-    send_near(
-        near,
-        lambda peer: x_ref.at[:, pl.ds(pl.multiple_of(peer * 128, 128), 128)],
-        lambda peer: recv_a.at[peer],
-        sems, 0,
-    )
-    recv_a[near] = x_ref[:, pl.ds(pl.multiple_of(near * 128, 128), 128)]
-
-    for step, distance in enumerate((1, 2, 4)):
-        greet(ring_sems.at[step], beside(distance, 0))
-        greet(ring_sems.at[step], beside(-distance, 0))
-        pl.semaphore_wait(ring_sems.at[step], 2)
-    greet(ring_sems.at[3], beside(-1, 0))
-    pl.semaphore_wait(ring_sems.at[3], 1)
     landed(recv_a.at[pl.ds(0, NEAR - 1)], sems.at[1])
 
     for pair in range(3):

time: 64.3 us -> 64.3 us (level)
  no operation moved by 1% of the time
where the time goes in v6:
time: 64.3 us; the launch traced here: 64.2 us
  Pallas kernels  63.6 us (99%)
    pallas_call x1, Pallas kernels, on_device(): pl.pallas_call(body, out_shape=pltpu.VMEM((STA_DEV, 2, 64), F32), in_spec...  63.6 us

profile of v6, /device:TPU:1, one launch (start us, length us, event | category | flops | bytes accessed | tf_op | source)
XLA Modules:
  0.0 64.2 jit_solution(7954100883906744900)
XLA Ops:
  0.0 63.6 %shard_map.55 = f32[6,2,64]{2,1,0:T(2,128)S(1)} custom-call(bf16[6,4,2,1024]{3,2,1,0:T(2,128)(2,1)} %x_hbm.1, s32[2,17]{1,0:T(2,128)} %bitcast.1, f32[17,6,6,512]{3,2,1,0:T(8,128)} %observed_ref.1, bf16[4,512,512]{2,1,0:T(8,128)(2,1)} %constant.4.clone.kernel_ref, bf16[8,256,128]{2,1,0:T(8,128)(2,1)} %constant.5.clone.maps_ref), custom_call_target="tpu_custom_call" | custom-call | tf_op jit(solution)/shard_map/pallas_call | solution.py:424
  63.6 0.6 copy.7
